TPU v7x, 64 devices: a 2x2x8 block of a 4x4x8 slice. The times are simulated.
64 devices in a mesh: dp: 4 (over x, y), tp: 16 (over z, core).
Axes of the slice: x: 2, y: 2, z: 8, core: 2. Of those that a mesh axis runs over, the one named last changes fastest.
The devices are a block of a 4x4x8 slice.
Arguments:
- hidden: bfloat16 [4, 2048, 2560], P('dp'), parts along dimension 0
- grad_out: bfloat16 [4, 2048, 2560], P('dp'), parts along dimension 0
- norm_gain: bfloat16 [2560], replicated
- w_query: bfloat16 [2560, 4096], P(None, 'tp')
- w_key: bfloat16 [2560, 1024], replicated
- w_value: bfloat16 [2560, 1024], replicated
- w_out: bfloat16 [4096, 2560], P('tp')
Outputs:
- output 1: bfloat16 [4, 2048, 2560], P('dp'), parts along dimension 0
- output 2: bfloat16 [4, 2048, 2560], P('dp'), parts along dimension 0
- output 3: float32 [10240], P('dp'), parts along dimension 0
- output 4: float32 [10240, 4096], P('dp', 'tp'), parts along dimension 0
- output 5: float32 [10240, 2048], P('dp', 'tp'), parts along dimension 0
- output 6: float32 [10240, 2048], P('dp', 'tp'), parts along dimension 0
- output 7: float32 [16384, 2560], P(('dp', 'tp')), parts along dimension 0
There are 4 independent parts. A program takes and returns all parts, laid end to end along the dimension named above; an argument that names none is the same for every part.
All inputs are finite; a program needn't handle non-finite values.
Results may differ from a plain program's by a relative error of at most 0.0098541.
Values sent between devices are 32-bit elements.
A program may use at most 768 MiB of HBM per device.

v0:
```python
import functools
import math
import jax
import jax.numpy as jnp
import numpy as np
from jax import lax
from jax.experimental import pallas as pl
from jax.experimental.pallas import tpu as pltpu
from jax.sharding import PartitionSpec as P

HEAD_DIM = 128
NORM_EPS = 1.0e-5
ROPE_BASE = 10000.0
MASK_VALUE = -1.0e30
SCORE_SCALE = 1.0 / math.sqrt(HEAD_DIM)
EXP2_SCALE = SCORE_SCALE * math.log2(math.e)
ROWS = 256
WIDE = 512
BF16 = jnp.bfloat16
F32 = jnp.float32
VMEM_LIMIT = 66 * 10**6


def dot(a, b, contract):
    return lax.dot_general(a, b, ((contract[:1], contract[1:]), ((), ())), preferred_element_type=F32)


def rope_tables(count):
    def table(positions):
        inv_freq = ROPE_BASE ** (-np.arange(0, HEAD_DIM, 2, dtype=np.float64) / HEAD_DIM)
        angles = positions[:, None] * inv_freq[None, :]
        cos_t = np.repeat(np.cos(angles), 2, axis=1)
        sin_t = np.stack([-np.sin(angles), np.sin(angles)], axis=-1).reshape(cos_t.shape)
        return np.stack([cos_t, sin_t]).astype(np.float32)
    return table(np.arange(ROWS, dtype=np.float64)), table(ROWS * np.arange(count, dtype=np.float64))


def rope_block(b, low_ref, high_ref):
    cos_b, sin_b = high_ref[0, pl.ds(b, 1), :], high_ref[1, pl.ds(b, 1), :]
    cos_l, sin_l = low_ref[0], low_ref[1]
    return cos_b * cos_l - sin_b * sin_l, sin_b * cos_l + cos_b * sin_l


def rotate(t, cos_t, sin_t):
    even = lax.broadcasted_iota(jnp.int32, t.shape, 1) % 2 == 0
    swapped = jnp.where(even, pltpu.roll(t, HEAD_DIM - 1, 1), pltpu.roll(t, 1, 1))
    return t * cos_t + swapped * sin_t


def front_kernel(kv_ref, x_ref, gain_ref, wq_ref, wk_ref, wv_ref, low_ref, high_ref,
                 n_ref, q_ref, k_ref, v_ref, wq32_ref, wqkv):
    i = pl.program_id(0)
    half = wq32_ref.shape[0]

    @pl.when(i == 0)
    def _():
        wqkv[:, :2 * HEAD_DIM] = wq_ref[...]
        wqkv[:, 2 * HEAD_DIM:3 * HEAD_DIM] = wk_ref[...]
        wqkv[:, 3 * HEAD_DIM:] = wv_ref[...]
        wq32_ref[...] = wq_ref[pl.ds(pl.multiple_of(kv_ref[1] * half, half), half), :].astype(F32)

    parts = []
    for r in range(0, WIDE, ROWS):
        rows = slice(r, r + ROWS)
        x = x_ref[rows, :].astype(F32)
        inv = lax.rsqrt(jnp.mean(x * x, axis=-1, keepdims=True) + NORM_EPS)
        n_ref[rows, :] = (x * inv * gain_ref[...].astype(F32)).astype(BF16)
        parts.append(rope_block(i * (WIDE // ROWS) + r // ROWS, low_ref, high_ref))
    qkv = dot(n_ref[...], wqkv[...], (1, 0))
    cos_t, sin_t = (jnp.concatenate([p[t] for p in parts], axis=0) for t in range(2))
    q0 = rotate(qkv[:, :HEAD_DIM], cos_t, sin_t).astype(BF16)
    q1 = rotate(qkv[:, HEAD_DIM:2 * HEAD_DIM], cos_t, sin_t).astype(BF16)
    k = rotate(qkv[:, 2 * HEAD_DIM:3 * HEAD_DIM], cos_t, sin_t).astype(BF16)
    v = qkv[:, 3 * HEAD_DIM:].astype(BF16)
    q_ref[:, :HEAD_DIM] = q0
    q_ref[:, HEAD_DIM:] = q1
    k_ref[...] = k
    v_ref[...] = v


def front(scalars, x, gain, wq, wk, wv, low, high):
    seq, d = x.shape
    row = lambda w: pl.BlockSpec((WIDE, w), lambda i, kv: (i, 0))
    whole = lambda shape: pl.BlockSpec(shape, lambda i, kv: (0,) * len(shape))
    head = pl.BlockSpec((d, HEAD_DIM), lambda i, kv: (0, kv[0]))
    widths = (d, 2 * HEAD_DIM, HEAD_DIM, HEAD_DIM)
    return pl.pallas_call(
        front_kernel,
        grid_spec=pltpu.PrefetchScalarGridSpec(
            num_scalar_prefetch=1, grid=(seq // WIDE,),
            in_specs=[row(d), whole(gain.shape), whole(wq.shape), head, head, whole(low.shape), whole(high.shape)],
            out_specs=[row(w) for w in widths] + [whole((d // 2, wq.shape[1]))],
            scratch_shapes=[pltpu.VMEM((d, 4 * HEAD_DIM), BF16)]),
        out_shape=[jax.ShapeDtypeStruct((seq, w), BF16) for w in widths] + [jax.ShapeDtypeStruct((d // 2, wq.shape[1]), F32)],
        compiler_params=pltpu.CompilerParams(vmem_limit_bytes=VMEM_LIMIT),
        cost_estimate=pl.CostEstimate(flops=2 * seq * d * 4 * HEAD_DIM, bytes_accessed=5 * seq * d, transcendentals=0),
        name='front')(scalars, x, gain, wq, wk, wv, low, high)


def attn_fwd_rows(c, q_ref, k_ref, v_ref, o_ref):
    lo, hi = c * WIDE, (c + 1) * WIDE

    def block(r, carry):
        rows = pl.ds(pl.multiple_of(lo + r * ROWS, ROWS), ROWS)
        q2 = jnp.concatenate([q_ref[rows, :HEAD_DIM], q_ref[rows, HEAD_DIM:]], axis=0)
        row_id = lax.broadcasted_iota(jnp.int32, (2 * ROWS, WIDE), 0) % ROWS + r * ROWS
        causal = row_id >= lax.broadcasted_iota(jnp.int32, (2 * ROWS, WIDE), 1)
        s_diag = jnp.where(causal, dot(q2, k_ref[lo:hi, :], (1, 1)), MASK_VALUE)
        m = jnp.max(s_diag, axis=-1, keepdims=True)
        if lo:
            s_pre = dot(q2, k_ref[:lo, :], (1, 1))
            m = jnp.maximum(m, jnp.max(s_pre, axis=-1, keepdims=True))
        p_diag = jnp.exp2((s_diag - m) * EXP2_SCALE)
        total = jnp.sum(p_diag, axis=-1, keepdims=True)
        if lo:
            p_pre = jnp.exp2((s_pre - m) * EXP2_SCALE)
            total = total + jnp.sum(p_pre, axis=-1, keepdims=True)
        scale = 1.0 / total
        o2 = dot((p_diag * scale).astype(BF16), v_ref[lo:hi, :], (1, 0))
        if lo:
            o2 = o2 + dot((p_pre * scale).astype(BF16), v_ref[:lo, :], (1, 0))
        o_ref[rows, :HEAD_DIM] = o2[:ROWS].astype(BF16)
        o_ref[rows, HEAD_DIM:] = o2[ROWS:].astype(BF16)
        return carry

    lax.fori_loop(0, WIDE // ROWS, block, 0)


def attn_bwd_rows(i, c, do_both, q_ref, k_ref, v_ref, low_ref, high_ref, dq32, dk_acc, dv_acc):
    lo, hi = c * WIDE, (c + 1) * WIDE
    rows = pl.ds(pl.multiple_of(i * ROWS, ROWS), ROWS)
    query_id = lax.broadcasted_iota(jnp.int32, (WIDE, ROWS), 1) + (i * ROWS - lo)
    causal = lax.broadcasted_iota(jnp.int32, (WIDE, ROWS), 0) <= query_id

    def one_head(head, carry):
        cols = pl.ds(pl.multiple_of(head * HEAD_DIM, HEAD_DIM), HEAD_DIM)
        q, do = q_ref[rows, cols], do_both[:, cols]
        k_all, v_all = k_ref[:hi, :], v_ref[:hi, :]
        s_t = dot(k_all, q, (1, 1))
        s_diag = jnp.where(causal, s_t[lo:], MASK_VALUE)
        s_t = jnp.concatenate([s_t[:lo], s_diag], axis=0) if lo else s_diag
        m = jnp.max(s_t, axis=0, keepdims=True)
        p = jnp.exp2((s_t - m) * EXP2_SCALE)
        p = p * (1.0 / jnp.sum(p, axis=0, keepdims=True))
        dp = dot(v_all, do, (1, 1))
        delta = jnp.sum(p * dp, axis=0, keepdims=True)
        ds = (p * (dp - delta) * SCORE_SCALE).astype(BF16)
        dv_acc[:hi, :] += dot(p.astype(BF16), do, (1, 0))
        dk_acc[:hi, :] += dot(ds, q, (1, 0))
        dq = dot(ds, k_all, (0, 0))
        cos_t, sin_t = rope_block(i, low_ref, high_ref)
        dq32[rows, cols] = rotate(dq, cos_t, -sin_t).astype(BF16).astype(F32)
        return carry

    lax.fori_loop(0, 2, one_head, 0)


SUBS = 4


def ring_kernel_setup(n):
    me = lax.axis_index('tp')
    chip, core = me // 2, me % 2
    right = (chip + 1) % n * 2 + core
    left = (chip + n - 1) % n * 2 + core
    sib = me + 1 - 2 * core
    barrier = pltpu.get_barrier_semaphore()
    for peer in (right, left, sib):
        pl.semaphore_signal(barrier, inc=1, device_id={'tp': peer}, device_id_type=pl.DeviceIdType.MESH)
    return chip, core, right, left, sib


def peers_ready():
    pl.semaphore_wait(pltpu.get_barrier_semaphore(), 3)


def remote(src, dst, send, recv, peer):
    return pltpu.make_async_remote_copy(src_ref=src, dst_ref=dst, send_sem=send, recv_sem=recv,
                                        device_id={'tp': peer}, device_id_type=pl.DeviceIdType.MESH)


def owned_rows(n, sub_rows, chip, sub):
    return pl.ds(pl.multiple_of((sub * n + chip) * sub_rows, sub_rows), sub_rows)


def ring_sum(n, place, extra, partial, ready, finish, rider, gather_rider, out_ref, gain_acc, bufs, sems):
    chip, core, right, left, sib = place
    rs_buf, ag_buf, sib_buf, obuf = bufs
    rs_send, rs_recv, ag_send, ag_recv, sib_send, sib_recv, out_sem, credit = sems
    width = rs_buf.shape[-1]
    block = out_ref.shape[0] // n
    sub_rows = block // SUBS
    half = 2 * width
    peers = (right, left)

    def part(slot_ref, sub, with_extra):
        return slot_ref.at[pl.ds(sub * sub_rows, sub_rows + (extra if with_extra and sub == SUBS - 1 else 0)), :]

    def rs_copy(s, sub, way):
        return remote(part(rs_buf.at[way, s], sub, False), part(rs_buf.at[way, s + 1], sub, False),
                      rs_send.at[way, s, sub], rs_recv.at[way, s, sub], peers[way])

    def ag_copy(s, sub, way):
        return remote(part(ag_buf.at[way, s], sub, True), part(ag_buf.at[way, s + 1], sub, True),
                      ag_send.at[way, s, sub], ag_recv.at[way, s, sub], peers[way])

    def sib_copy(s, sub, way):
        rows = sub_rows + (extra if sub == SUBS - 1 else 0)
        k = SUBS * s + sub
        return remote(part(ag_buf.at[way, s], sub, True), sib_buf.at[way, k % (2 * SUBS), pl.ds(0, rows), :],
                      sib_send.at[way, k], sib_recv.at[way, k], sib)

    def my_part(dest, sub, way):
        return partial(owned_rows(n, sub_rows, dest, sub), way)

    def dest_of(s, way):
        return (chip + n - 1 - s) % n if way == 0 else (chip + 1 + s) % n

    def local(ref, sub):
        return pl.ds(sub * sub_rows, sub_rows)

    for sub in range(SUBS):
        ready(sub)
        for way in range(2):
            rs_buf[way, 0, local(rs_buf, sub), :] = my_part(dest_of(0, way), sub, way)
            rs_copy(0, sub, way).start()

    def rs_step(s, carry):
        for sub in range(SUBS):
            for way in range(2):
                term = my_part(dest_of(s, way), sub, way)
                rs_copy(s - 1, sub, way).wait_recv()
                rs_buf[way, s, local(rs_buf, sub), :] += term
                rs_copy(s, sub, way).start()
            if sub == 0:
                rider(s)
        return carry

    lax.fori_loop(1, n - 1, rs_step, 0)

    def out_copy(whose, s, sub, way):
        b = (chip + n - s) % n if way == 0 else (chip + s) % n
        col = (core if whose == 0 else 1 - core) * half + way * width
        dst = out_ref.at[owned_rows(n, sub_rows, b, sub), pl.ds(pl.multiple_of(col, 128), width)]
        return pltpu.make_async_copy(obuf.at[whose, sub, way], dst, out_sem.at[whose, sub, way])

    def emit(whose, s, sub, way, values):
        @pl.when(s >= 1)
        def _():
            out_copy(whose, s - 1, sub, way).wait()
        obuf[whose, sub, way] = values.astype(BF16)
        out_copy(whose, s, sub, way).start()

    def own_chunk(s, sub, forward):
        @pl.when(s >= 2)
        def _():
            pl.semaphore_wait(credit, 1)
        for way in range(2):
            if forward:
                ag_copy(s, sub, way).start()
            sib_copy(s, sub, way).start()
        for way in range(2):
            emit(0, s, sub, way, ag_buf[way, s, local(ag_buf, sub), :])
            if extra and sub == SUBS - 1:
                gain_acc[0, way] += ag_buf[way, s, pl.ds(block, extra), :]

    def sib_chunk(s, sub):
        k = SUBS * s + sub
        for way in range(2):
            sib_copy(s, sub, way).wait_recv()
            emit(1, s, sub, way, sib_buf[way, k % (2 * SUBS), pl.ds(0, sub_rows), :])
            if extra and sub == SUBS - 1:
                gain_acc[1, way] += sib_buf[way, k % (2 * SUBS), pl.ds(sub_rows, extra), :]

        @pl.when(s < n - 2)
        def _():
            pl.semaphore_signal(credit, inc=1, device_id={'tp': sib}, device_id_type=pl.DeviceIdType.MESH)

    for sub in range(SUBS):
        terms = [my_part(chip, sub, way) for way in range(2)]
        for way in range(2):
            rs_copy(n - 2, sub, way).wait_recv()
        finish(sub, [rs_buf[way, n - 1, local(rs_buf, sub), :] + terms[way] for way in range(2)])
        own_chunk(0, sub, True)
        if sub:
            sib_chunk(0, sub - 1)

    def ag_step(s, carry):
        for sub in range(SUBS):
            for way in range(2):
                ag_copy(s - 1, sub, way).wait_recv()
            own_chunk(s, sub, True)
            if sub == 0:
                sib_chunk(s - 1, SUBS - 1)
                gather_rider(s)
            else:
                sib_chunk(s, sub - 1)
        return carry

    lax.fori_loop(1, n - 1, ag_step, 0)
    last = n - 1
    for sub in range(SUBS):
        for way in range(2):
            ag_copy(last - 1, sub, way).wait_recv()
        own_chunk(last, sub, False)
        if sub == 0:
            sib_chunk(last - 1, SUBS - 1)
        else:
            sib_chunk(last, sub - 1)
    sib_chunk(last, SUBS - 1)
    for sub in range(SUBS):
        for way in range(2):
            for whose in range(2):
                out_copy(whose, last, sub, way).wait()

    def drain(s, carry):
        for sub in range(SUBS):
            for way in range(2):
                rs_copy(s, sub, way).wait_send()
                ag_copy(s, sub, way).wait_send()
                sib_copy(s, sub, way).wait_send()
        return carry

    lax.fori_loop(0, n - 1, drain, 0)
    for sub in range(SUBS):
        for way in range(2):
            sib_copy(last, sub, way).wait_send()


def ring_scratch(n, seq, d_model, extra):
    width, block = d_model // 4, seq // n
    sub_rows = block // SUBS
    dma = pltpu.SemaphoreType.DMA
    return [
        pltpu.VMEM((2, n, block, width), F32),
        pltpu.VMEM((2, n, block + extra, width), F32),
        pltpu.VMEM((2, 2 * SUBS, sub_rows + extra, width), F32),
        pltpu.VMEM((2, SUBS, 2, sub_rows, width), BF16),
        dma((2, n - 1, SUBS)), dma((2, n - 1, SUBS)), dma((2, n - 1, SUBS)), dma((2, n - 1, SUBS)),
        dma((2, SUBS * n)), dma((2, SUBS * n)), dma((2, SUBS, 2)), pltpu.SemaphoreType.REGULAR,
    ]


def out_kernel(n, wo_ref, q_ref, k_ref, v_ref, low_ref, high_ref, x_ref, dout_ref,
               out_ref, o_ref, dlhs_ref, lhs, rhs, x_rows, dout_rows, do_blk, dk_acc, x32, dkv32, wo32, o_got, wo_got, dq_got, dkv_got,
               row_sem, dout_sem, swap_send, swap_recv, o_send, o_recv, *ring):
    bufs, sems = ring[:4], ring[4:]
    place = ring_kernel_setup(n)
    chip, core, right, left, sib = place
    width = bufs[0].shape[-1]
    half = 2 * width
    block = x_rows.shape[0]
    sub_rows = block // SUBS
    inner = o_ref.shape[1]
    wide = n * sub_rows
    my_cols = pl.ds(pl.multiple_of(core * half, 128), half)

    def x_copy(sub):
        return pltpu.make_async_copy(x_ref.at[owned_rows(n, sub_rows, chip, sub), my_cols],
                                     x_rows.at[pl.ds(sub * sub_rows, sub_rows), :], row_sem.at[sub])

    def dout_copy(i):
        return pltpu.make_async_copy(dout_ref.at[pl.ds(pl.multiple_of(i * ROWS, ROWS), ROWS), :], dout_rows.at[i % 2], dout_sem.at[i % 2])

    swaps = [remote(src, dst, swap_send.at[k], swap_recv.at[k], sib)
             for k, (src, dst) in enumerate([(wo32, wo_got), (x32, dq_got), (dkv32, dkv_got)])]

    def o_swap(w):
        rows = pl.ds(w * wide, wide)
        return remote(x32.at[rows, :], o_got.at[rows, :], o_send.at[w], o_recv.at[w], sib)

    def forward(w):
        rows = pl.ds(w * wide, wide)
        attn_fwd_rows(w, q_ref, k_ref, v_ref, o_ref)
        x32[rows, :] = o_ref[rows, :].astype(F32)
        o_swap(w).start()
        lhs[rows, :inner] = o_ref[rows, :]

    for sub in range(SUBS):
        x_copy(sub).start()
    dout_copy(0).start()
    wo32[...] = wo_ref[:, pl.ds(pl.multiple_of((1 - core) * half, 128), half)].astype(F32)
    peers_ready()
    swaps[0].start()
    forward(0)
    rhs[:inner, :] = wo_ref[:, my_cols]
    swaps[0].wait()
    rhs[inner:, :] = wo_got[...].astype(BF16)

    def ready(sub):
        if sub + 1 < SUBS:
            forward(sub + 1)
        o_swap(sub).wait()
        rows = pl.ds(sub * wide, wide)
        lhs[rows, inner:] = o_got[rows, :].astype(BF16)
        if sub == SUBS - 1:
            dk_acc[...] = jnp.zeros_like(dk_acc)
            dkv32[:, HEAD_DIM:] = jnp.zeros_like(dk_acc)

    def partial(rows, way):
        return dot(lhs[rows, :], rhs[:, way * width:(way + 1) * width], (1, 0))

    def finish(sub, sums):
        x_copy(sub).wait()
        for way in range(2):
            rows = pl.ds(sub * sub_rows, sub_rows)
            bufs[1][way, 0, rows, :] = sums[way] + x_rows[rows, way * width:(way + 1) * width].astype(F32)

    dv_acc = dkv32.at[:, pl.ds(HEAD_DIM, HEAD_DIM)]
    count = q_ref.shape[0] // ROWS
    per_wide = WIDE // ROWS

    def ride(i, wides):
        dout_copy(i).wait()

        @pl.when(i + 1 < count)
        def _():
            dout_copy(i + 1).start()
        do_blk[...] = dot(dout_rows[i % 2], wo_ref[...], (1, 1)).astype(BF16)
        for c in wides:
            pl.when(i // per_wide == c)(
                lambda c=c: attn_bwd_rows(i, c, do_blk, q_ref, k_ref, v_ref, low_ref, high_ref, x32, dk_acc, dv_acc))

    early = n - 2

    def rider(step):
        ride(step - 1, range((early - 1) // per_wide + 1))

    def gather_rider(step):
        @pl.when(step <= count - early)
        def _():
            ride(early - 1 + step, range(early // per_wide, count // per_wide))

        @pl.when(step == count - early + 1)
        def _():
            def turn_back(b, carry):
                rows = pl.ds(pl.multiple_of(b * ROWS, ROWS), ROWS)
                cos_t, sin_t = rope_block(b, low_ref, high_ref)
                dkv32[rows, :HEAD_DIM] = rotate(dk_acc[rows, :], cos_t, -sin_t)
                return carry
            lax.fori_loop(0, count, turn_back, 0)
            swaps[1].start()
            swaps[2].start()

        @pl.when(step == n - 2)
        def _():
            swaps[1].wait()
            swaps[2].wait()
            dlhs_ref[:, :inner] = x32[...].astype(BF16)
            dlhs_ref[:, inner:2 * inner] = (dkv32[...] + dkv_got[...]).astype(BF16)
            dlhs_ref[:, 2 * inner:] = dq_got[...].astype(BF16)

    ring_sum(n, place, 0, partial, ready, finish, rider, gather_rider, out_ref, None, bufs, sems)


def grad_kernel(n, lhs, o_ref, wqsib_ref, gain_ref, wq_ref, wk_ref, wv_ref, x_ref, dout_ref, n_ref,
                out_ref, gsum_ref, dw_ref, dwo_ref, n_blk, dout_blk, dw_blk, dwo_blk, blk_sem, dw_sem, rhs, gain, x_rows, dout_rows, unit_buf, stat_buf, gain_acc, row_sem, stat_send, stat_recv, *ring):
    bufs, sems = ring[:4], ring[4:]
    place = ring_kernel_setup(n)
    chip, core, right, left, sib = place
    width = bufs[0].shape[-1]
    block = x_rows.shape[0]
    inner = wq_ref.shape[1]
    half = 2 * width
    col = pl.multiple_of(core * half, 128)
    head_cols = pl.ds(pl.multiple_of(chip * HEAD_DIM, HEAD_DIM), HEAD_DIM)
    sub_rows = block // SUBS
    rows_copies = []
    for sub in range(SUBS):
        src, dst = owned_rows(n, sub_rows, chip, sub), pl.ds(sub * sub_rows, sub_rows)
        rows_copies += [pltpu.make_async_copy(x_ref.at[src, :], x_rows.at[dst, :], row_sem.at[3 + 2 * sub]),
                        pltpu.make_async_copy(dout_ref.at[src, pl.ds(col, half)], dout_rows.at[dst, :], row_sem.at[4 + 2 * sub])]
    weights = [
        pltpu.make_async_copy(wq_ref.at[pl.ds(col, half), :], rhs.at[:, pl.ds(0, inner)], row_sem.at[0]),
        pltpu.make_async_copy(wk_ref.at[pl.ds(col, half), head_cols], rhs.at[:, pl.ds(inner, HEAD_DIM)], row_sem.at[1]),
        pltpu.make_async_copy(wv_ref.at[pl.ds(col, half), head_cols], rhs.at[:, pl.ds(inner + HEAD_DIM, HEAD_DIM)], row_sem.at[2]),
    ]
    count = n_ref.shape[1] // ROWS

    def loads(j):
        cols = pl.ds(pl.multiple_of(j * ROWS, ROWS), ROWS)
        return [pltpu.make_async_copy(n_ref.at[:, cols], n_blk.at[j % 2], blk_sem.at[0, j % 2]),
                pltpu.make_async_copy(dout_ref.at[:, cols], dout_blk.at[j % 2], blk_sem.at[1, j % 2])]

    def stores(j):
        cols = pl.ds(pl.multiple_of(j * ROWS, ROWS), ROWS)
        return [pltpu.make_async_copy(dw_blk.at[j % 2], dw_ref.at[cols, :], dw_sem.at[0, j % 2]),
                pltpu.make_async_copy(dwo_blk.at[j % 2], dwo_ref.at[:, cols], dw_sem.at[1, j % 2])]

    def weight_block(j):
        for copy in loads(j):
            copy.wait()

        @pl.when(j + 1 < count)
        def _():
            for copy in loads(j + 1):
                copy.start()

        @pl.when(j >= 2)
        def _():
            for copy in stores(j - 2):
                copy.wait()
        dw_blk[j % 2] = dot(n_blk[j % 2], lhs[:, :2 * inner], (0, 0))
        dwo_blk[j % 2] = dot(o_ref[...], dout_blk[j % 2], (0, 0))
        for copy in stores(j):
            copy.start()

    for copy in weights + rows_copies + loads(0):
        copy.start()
    rhs[:, inner + 2 * HEAD_DIM:] = wqsib_ref[...].astype(BF16)
    gain[...] = gain_ref[:, pl.ds(col, half)].astype(F32)
    for copy in weights:
        copy.wait()
    peers_ready()
    gain_acc[...] = jnp.zeros_like(gain_acc)

    def partial(rows, way):
        return dot(lhs[rows, :], rhs[way * width:(way + 1) * width, :], (1, 1))

    def prepare(sub):
        rows = pl.ds(sub * sub_rows, sub_rows)
        x = x_rows[rows, :].astype(F32)
        inv = lax.rsqrt(jnp.mean(x * x, axis=-1, keepdims=True) + NORM_EPS)
        stat_buf[2, rows, :] = jnp.broadcast_to(inv, (sub_rows, HEAD_DIM))
        mine = x_rows[rows, pl.ds(col, half)].astype(F32)
        unit_buf[rows, :] = mine * inv

    def ready(sub):
        if sub == SUBS - 1:
            for copy in rows_copies:
                copy.wait()

    def rider(step):
        @pl.when(step == 1)
        def _():
            for sub in range(SUBS):
                prepare(sub)
        pl.when(step - 1 < count)(lambda: weight_block(step - 1))

    def gather_rider(step):
        pl.when(step + n - 3 < count)(lambda: weight_block(step + n - 3))

    def stat_copy(sub):
        rows = pl.ds(sub * sub_rows, sub_rows)
        return remote(stat_buf.at[0, rows, :], stat_buf.at[1, rows, :], stat_send.at[sub], stat_recv.at[sub], sib)

    def finish(sub, sums):
        rows = pl.ds(sub * sub_rows, sub_rows)
        ag_buf = bufs[1]
        total = jnp.zeros((sub_rows, 1), F32)
        for way in range(2):
            cols = slice(way * width, (way + 1) * width)
            unit = unit_buf[rows, cols]
            prod = sums[way] * unit
            total = total + jnp.sum(prod * gain[:, cols], axis=-1, keepdims=True)
            gsum = jnp.sum(prod.reshape(sub_rows // 8, 8, width), axis=0)
            ag_buf[way, 0, pl.ds(block, 8), :] = gsum if sub == 0 else gsum + ag_buf[way, 0, pl.ds(block, 8), :]
            ag_buf[way, 0, rows, :] = sums[way]
        stat_buf[0, rows, :] = jnp.broadcast_to(total, (sub_rows, HEAD_DIM))
        stat_copy(sub).start()
        stat_copy(sub).wait()
        mean = (stat_buf[0, rows, 0:1] + stat_buf[1, rows, 0:1]) * (1.0 / (2 * half))
        inv = stat_buf[2, rows, 0:1]
        for way in range(2):
            cols = slice(way * width, (way + 1) * width)
            scaled = ag_buf[way, 0, rows, :] * gain[:, cols]
            ag_buf[way, 0, rows, :] = dout_rows[rows, cols].astype(F32) + inv * (scaled - unit_buf[rows, cols] * mean)

    ring_sum(n, place, 8, partial, ready, finish, rider, gather_rider, out_ref, gain_acc, bufs, sems)
    for j in (count - 2, count - 1):
        for copy in stores(j):
            copy.wait()
    for way in range(2):
        gsum_ref[core, way] = jnp.sum(gain_acc[0, way], axis=0, keepdims=True)
        gsum_ref[1 - core, way] = jnp.sum(gain_acc[1, way], axis=0, keepdims=True)


def final_kernel(*refs):
    half = len(refs) // 2
    for src, dst in zip(refs[:half], refs[half:]):
        dst[...] = src[...]


def final(out, gh, dw, dwo):
    seq, d = out.shape
    inner = dwo.shape[0]
    steps = seq // ROWS
    row = lambda a: pl.BlockSpec((a.shape[0] // steps, a.shape[1]), lambda j: (j, 0))
    part = lambda w, at: pl.BlockSpec((d // steps, w), lambda j: (j, at))
    shape = jax.ShapeDtypeStruct
    return pl.pallas_call(
        final_kernel, grid=(steps,),
        in_specs=[row(out), row(gh), part(inner, 0), part(HEAD_DIM, inner // HEAD_DIM), part(HEAD_DIM, inner // HEAD_DIM + 1), row(dwo)],
        out_specs=[row(out), row(gh), part(inner, 0), part(HEAD_DIM, 0), part(HEAD_DIM, 0), row(dwo)],
        out_shape=[shape(out.shape, BF16), shape(gh.shape, BF16), shape((d, inner), F32), shape((d, HEAD_DIM), F32),
                   shape((d, HEAD_DIM), F32), shape(dwo.shape, F32)],
        compiler_params=pltpu.CompilerParams(vmem_limit_bytes=VMEM_LIMIT),
        cost_estimate=pl.CostEstimate(flops=seq * d, bytes_accessed=12 * seq * d, transcendentals=0),
        name='final')(out, gh, dw, dw, dw, dwo)


def out_sum(n, wo, q, k, v, low, high, x, dout):
    seq, d_model = x.shape
    half, block, inner = d_model // 2, seq // n, q.shape[1]
    vmem, hbm = pl.BlockSpec(memory_space=pltpu.VMEM), pl.BlockSpec(memory_space=pl.ANY)
    shape = jax.ShapeDtypeStruct
    dma = pltpu.SemaphoreType.DMA
    rows32 = pltpu.VMEM((seq, inner), F32)
    wide32 = pltpu.VMEM((inner, half), F32)
    return pl.pallas_call(
        functools.partial(out_kernel, n),
        out_shape=[shape((seq, d_model), BF16), shape(q.shape, BF16), shape((seq, 2 * inner + 2 * HEAD_DIM), BF16)],
        in_specs=[vmem] * 6 + [hbm] * 2, out_specs=[hbm, vmem, vmem],
        scratch_shapes=[pltpu.VMEM((seq, 2 * inner), BF16), pltpu.VMEM((2 * inner, half), BF16),
                        pltpu.VMEM((block, half), BF16), pltpu.VMEM((2, ROWS, d_model), BF16), pltpu.VMEM((ROWS, inner), BF16),
                        pltpu.VMEM((seq, HEAD_DIM), F32), rows32, rows32, wide32, rows32, wide32, rows32, rows32,
                        dma((SUBS,)), dma((2,)), dma((3,)), dma((3,)), dma((SUBS,)), dma((SUBS,))]
        + ring_scratch(n, seq, d_model, 0),
        compiler_params=pltpu.CompilerParams(collective_id=1, has_side_effects=True, vmem_limit_bytes=VMEM_LIMIT),
        cost_estimate=pl.CostEstimate(flops=10 * seq * seq * HEAD_DIM, bytes_accessed=4 * seq * d_model, transcendentals=seq * seq),
        name='out_sum')(wo, q, k, v, low, high, x, dout)


def grad_sum(n, dlhs, o, wq_sib, gain, wq, wk, wv, x, dout, normed):
    seq, d_model = x.shape
    half, block, width = d_model // 2, seq // n, d_model // 4
    kdim, inner = dlhs.shape[1], o.shape[1]
    vmem, hbm = pl.BlockSpec(memory_space=pltpu.VMEM), pl.BlockSpec(memory_space=pl.ANY)
    shape = jax.ShapeDtypeStruct
    dma = pltpu.SemaphoreType.DMA
    return pl.pallas_call(
        functools.partial(grad_kernel, n),
        out_shape=[shape((seq, d_model), BF16), shape((2, 2, 1, width), F32), shape((d_model, 2 * inner), F32), shape((inner, d_model), F32)],
        in_specs=[vmem] * 4 + [hbm] * 6, out_specs=[hbm, vmem, hbm, hbm],
        scratch_shapes=[pltpu.VMEM((2, seq, ROWS), BF16), pltpu.VMEM((2, seq, ROWS), BF16),
                        pltpu.VMEM((2, ROWS, 2 * inner), F32), pltpu.VMEM((2, inner, ROWS), F32), dma((2, 2)), dma((2, 2)),
                        pltpu.VMEM((half, kdim), BF16), pltpu.VMEM((1, half), F32),
                        pltpu.VMEM((block, d_model), BF16), pltpu.VMEM((block, half), BF16), pltpu.VMEM((block, half), F32),
                        pltpu.VMEM((3, block, HEAD_DIM), F32), pltpu.VMEM((2, 2, 8, width), F32),
                        dma((3 + 2 * SUBS,)), dma((SUBS,)), dma((SUBS,))]
        + ring_scratch(n, seq, d_model, 8),
        compiler_params=pltpu.CompilerParams(collective_id=2, has_side_effects=True, vmem_limit_bytes=VMEM_LIMIT),
        cost_estimate=pl.CostEstimate(flops=4 * seq * kdim * half, bytes_accessed=4 * seq * d_model, transcendentals=0),
        name='grad_sum')(dlhs, o, wq_sib, gain, wq, wk, wv, x, dout, normed)


def solution(mesh):
    tp_size = mesh.shape['tp']
    chips = tp_size // 2
    swap = [(source, source ^ 1) for source in range(tp_size)]

    def block_fn(hidden, grad_out, norm_gain, w_query, w_key, w_value, w_out):
        batch, seq_len, d_model = hidden.shape
        half = d_model // 2
        tp_index = lax.axis_index('tp')
        kv_index, core = tp_index // 2, tp_index % 2
        low, high = rope_tables(seq_len // ROWS)
        x, dout = hidden[0], grad_out[0]
        gain = norm_gain[None, :]
        scalars = jnp.stack([kv_index, 1 - core])
        n, q, k, v, wq32 = front(scalars, x, gain, w_query, w_key, w_value, low, high)
        wq_sib = lax.ppermute(wq32, 'tp', swap)
        out, o, dlhs = out_sum(chips, w_out, q, k, v, low, high, x, dout)
        gh, gain_sum, dw, dwo = grad_sum(chips, dlhs, o, wq_sib, gain, w_query, w_key, w_value, x, dout, n)
        out, gh, grad_w_query, grad_w_key, grad_w_value, grad_w_out = final(out, gh, dw, dwo)
        return out[None], gh[None], gain_sum.reshape(-1), grad_w_query, grad_w_key, grad_w_value, grad_w_out

    act_spec = P('dp', None, None)
    return jax.shard_map(
        block_fn, mesh=mesh,
        in_specs=(act_spec, act_spec, P(None), P(None, 'tp'), P(None, None), P(None, None), P('tp', None)),
        out_specs=(act_spec, act_spec, P('dp'), P('dp', 'tp'), P('dp', 'tp'), P('dp', 'tp'), P(('dp', 'tp'), None)),
        check_vma=False)
```

profile of v0, /device:TPU:21, one launch (start us, length us, event | category | flops | bytes accessed | tf_op | source)
XLA Modules:
  0.0 480.7 jit_solution(7058575587962018164)
XLA Ops:
  0.6 1.3 broadcast_in_dim.9.gain_ref
  1.9 0.6 pad_add_fusion.kv_ref
  2.5 14.7 %front.1 = (bf16[2048,2560]{1,0:T(8,128)(2,1)}, bf16[2048,256]{1,0:T(8,128)(2,1)}, bf16[2048,128]{1,0:T(8,128)(2,1)}, bf16[2048,128]{1,0:T(8,128)(2,1)}, f32[1280,256]{1,0:T(8,128)}) custom-call(s32[2]{0:T(128)} %pad_add_fusion.kv_ref, bf16[2048,2560]{1,0:T(8,128)(2,1)} %bitcast.6, bf16[1,2560]{1,0:T(2,128)(2,1)} %broadcast_in_dim.9.gain_ref, ...), custom_call_target="tpu_custom_call" | custom-call | flops 5368709120 | bytes 26214400 | tf_op jit(solution)/shard_map/front/pallas_call | solution.py:87
  17.2 4.7 collective-permute-start
  22.0 223.0 %out_sum.1 = (bf16[2048,2560]{1,0:T(8,128)(2,1)}, bf16[2048,256]{1,0:T(8,128)(2,1)}, bf16[2048,768]{1,0:T(8,128)(2,1)}) custom-call(bf16[256,2560]{1,0:T(8,128)(2,1)} %wo_ref.1, bf16[2048,256]{1,0:T(8,128)(2,1)} %get-tuple-element.25.q_ref, bf16[2048,128]{1,0:T(8,128)(2,1)} %get-tuple-element.26.k_ref, bf16[2048,128]{1,0:T(8,128)(2,1)} %get-tuple-element.27.v_ref, ...), custom_call_target="tpu_custom_call" | custom-call | flops 5368709120 | bytes 20971520 | tf_op jit(solution)/shard_map/out_sum/pallas_call | solution.py:610
  245.0 0.0 collective-permute-done.wqsib_ref
  245.0 214.3 %grad_sum.1 = (bf16[2048,2560]{1,0:T(8,128)(2,1)}, f32[2,2,1,640]{3,2,1,0:T(1,128)}, f32[2560,512]{1,0:T(8,128)}, f32[256,2560]{1,0:T(8,128)}) custom-call(bf16[2048,768]{1,0:T(8,128)(2,1)} %get-tuple-element.29.lhs, bf16[2048,256]{1,0:T(8,128)(2,1)} %get-tuple-element.30.o_ref, f32[1280,256]{1,0:T(8,128)} %collective-permute-done.wqsib_ref, ...), custom_call_target="tpu_custom_call" | custom-call | flops 8053063680 | bytes 20971520 | tf_op jit(solution)/shard_map/grad_sum/pallas_call | solution.py:631
  459.3 0.7 reduce
  460.0 0.6 reshape.17
  460.6 19.9 %final.1 = (bf16[2048,2560]{1,0:T(8,128)(2,1)}, bf16[2048,2560]{1,0:T(8,128)(2,1)}, f32[2560,256]{1,0:T(8,128)}, f32[2560,128]{1,0:T(8,128)}, f32[2560,128]{1,0:T(8,128)}, /*index=5*/f32[256,2560]{1,0:T(8,128)}) custom-call(bf16[2048,2560]{1,0:T(8,128)(2,1)} %get-tuple-element.28.refs_0_, bf16[2048,2560]{1,0:T(8,128)(2,1)} %get-tuple-element.33.refs_1_, ...), custom_call_target="tpu_custom_call" | custom-call | flops 5242880 | bytes 62914560 | tf_op jit(solution)/shard_map/final/pallas_call | solution.py:591
Async XLA Ops:
  17.2 227.7 %collective-permute-start = (f32[1280,256]{1,0:T(8,128)}, f32[1280,256]{1,0:T(8,128)}, u32[]{:S(2)}, u32[]{:S(2)}) collective-permute-start(f32[1280,256]{1,0:T(8,128)} %get-tuple-element.31), channel_id=1, source_target_pairs={{0,1},{1,0},{2,3},{3,2},{4,5},{5,4},{6,7},{7,6},{8,9},{9,8},{10,11... | collective-permute-start | bytes 3932168 | tf_op jit(solution)/shard_map/ppermute | solution.py:662
where the time goes:
time: 481 us
  Pallas kernels  472 us (98%)
    pallas_call x1, Pallas kernels, out_sum(): pl.pallas_call(functools.partial(out_kernel, n), out_shape=[shape((seq, d...  223 us
    pallas_call x1, Pallas kernels, grad_sum(): pl.pallas_call(functools.partial(grad_kernel, n), out_shape=[shape((seq,...  214 us
    pallas_call x1, Pallas kernels, final(): pl.pallas_call(final_kernel, grid=(steps,), in_specs=[row(out), row(gh),...  19.9 us
    pallas_call x1, Pallas kernels, front(): pl.pallas_call(front_kernel, grid_spec=pltpu.PrefetchScalarGridSpec(num_s...  14.7 us
  transfers between devices with their start and end apart: 1, of which 0 were waited for; matrix products, arithmetic and copies ran while one was open for 0% of the time, Pallas kernels for 46%

commit v1 on v0

--- a/solution.py
+++ b/solution.py
@@ -48,15 +48,17 @@
 
 
 def front_kernel(kv_ref, x_ref, gain_ref, wq_ref, wk_ref, wv_ref, low_ref, high_ref,
-                 n_ref, q_ref, k_ref, v_ref, wq32_ref, wqkv):
+                 n_ref, q_ref, k_ref, v_ref, wq32_ref, gain_row, wqkv):
     i = pl.program_id(0)
     half = wq32_ref.shape[0]
+    gain = gain_ref[...].astype(F32).reshape(gain_row.shape)
 
     @pl.when(i == 0)
     def _():
         wqkv[:, :2 * HEAD_DIM] = wq_ref[...]
         wqkv[:, 2 * HEAD_DIM:3 * HEAD_DIM] = wk_ref[...]
         wqkv[:, 3 * HEAD_DIM:] = wv_ref[...]
+        gain_row[...] = gain
         wq32_ref[...] = wq_ref[pl.ds(pl.multiple_of(kv_ref[1] * half, half), half), :].astype(F32)
 
     parts = []
@@ -64,7 +66,7 @@
         rows = slice(r, r + ROWS)
         x = x_ref[rows, :].astype(F32)
         inv = lax.rsqrt(jnp.mean(x * x, axis=-1, keepdims=True) + NORM_EPS)
-        n_ref[rows, :] = (x * inv * gain_ref[...].astype(F32)).astype(BF16)
+        n_ref[rows, :] = (x * inv * gain).astype(BF16)
         parts.append(rope_block(i * (WIDE // ROWS) + r // ROWS, low_ref, high_ref))
     qkv = dot(n_ref[...], wqkv[...], (1, 0))
     cos_t, sin_t = (jnp.concatenate([p[t] for p in parts], axis=0) for t in range(2))
@@ -89,9 +91,9 @@
         grid_spec=pltpu.PrefetchScalarGridSpec(
             num_scalar_prefetch=1, grid=(seq // WIDE,),
             in_specs=[row(d), whole(gain.shape), whole(wq.shape), head, head, whole(low.shape), whole(high.shape)],
-            out_specs=[row(w) for w in widths] + [whole((d // 2, wq.shape[1]))],
+            out_specs=[row(w) for w in widths] + [whole((d // 2, wq.shape[1])), whole((1, d))],
             scratch_shapes=[pltpu.VMEM((d, 4 * HEAD_DIM), BF16)]),
-        out_shape=[jax.ShapeDtypeStruct((seq, w), BF16) for w in widths] + [jax.ShapeDtypeStruct((d // 2, wq.shape[1]), F32)],
+        out_shape=[jax.ShapeDtypeStruct((seq, w), BF16) for w in widths] + [jax.ShapeDtypeStruct((d // 2, wq.shape[1]), F32), jax.ShapeDtypeStruct((1, d), F32)],
         compiler_params=pltpu.CompilerParams(vmem_limit_bytes=VMEM_LIMIT),
         cost_estimate=pl.CostEstimate(flops=2 * seq * d * 4 * HEAD_DIM, bytes_accessed=5 * seq * d, transcendentals=0),
         name='front')(scalars, x, gain, wq, wk, wv, low, high)
@@ -126,33 +128,29 @@
     lax.fori_loop(0, WIDE // ROWS, block, 0)
 
 
-def attn_bwd_rows(i, c, do_both, q_ref, k_ref, v_ref, low_ref, high_ref, dq32, dk_acc, dv_acc):
+def attn_bwd_rows(i, head, c, do_both, q_ref, k_ref, v_ref, low_ref, high_ref, dq32, dk_acc, dv_acc):
     lo, hi = c * WIDE, (c + 1) * WIDE
     rows = pl.ds(pl.multiple_of(i * ROWS, ROWS), ROWS)
     query_id = lax.broadcasted_iota(jnp.int32, (WIDE, ROWS), 1) + (i * ROWS - lo)
     causal = lax.broadcasted_iota(jnp.int32, (WIDE, ROWS), 0) <= query_id
 
-    def one_head(head, carry):
-        cols = pl.ds(pl.multiple_of(head * HEAD_DIM, HEAD_DIM), HEAD_DIM)
-        q, do = q_ref[rows, cols], do_both[:, cols]
-        k_all, v_all = k_ref[:hi, :], v_ref[:hi, :]
-        s_t = dot(k_all, q, (1, 1))
-        s_diag = jnp.where(causal, s_t[lo:], MASK_VALUE)
-        s_t = jnp.concatenate([s_t[:lo], s_diag], axis=0) if lo else s_diag
-        m = jnp.max(s_t, axis=0, keepdims=True)
-        p = jnp.exp2((s_t - m) * EXP2_SCALE)
-        p = p * (1.0 / jnp.sum(p, axis=0, keepdims=True))
-        dp = dot(v_all, do, (1, 1))
-        delta = jnp.sum(p * dp, axis=0, keepdims=True)
-        ds = (p * (dp - delta) * SCORE_SCALE).astype(BF16)
-        dv_acc[:hi, :] += dot(p.astype(BF16), do, (1, 0))
-        dk_acc[:hi, :] += dot(ds, q, (1, 0))
-        dq = dot(ds, k_all, (0, 0))
-        cos_t, sin_t = rope_block(i, low_ref, high_ref)
-        dq32[rows, cols] = rotate(dq, cos_t, -sin_t).astype(BF16).astype(F32)
-        return carry
-
-    lax.fori_loop(0, 2, one_head, 0)
+    cols = pl.ds(pl.multiple_of(head * HEAD_DIM, HEAD_DIM), HEAD_DIM)
+    q, do = q_ref[rows, cols], do_both[:, cols]
+    k_all, v_all = k_ref[:hi, :], v_ref[:hi, :]
+    s_t = dot(k_all, q, (1, 1))
+    s_diag = jnp.where(causal, s_t[lo:], MASK_VALUE)
+    s_t = jnp.concatenate([s_t[:lo], s_diag], axis=0) if lo else s_diag
+    m = jnp.max(s_t, axis=0, keepdims=True)
+    p = jnp.exp2((s_t - m) * EXP2_SCALE)
+    p = p * (1.0 / jnp.sum(p, axis=0, keepdims=True))
+    dp = dot(v_all, do, (1, 1))
+    delta = jnp.sum(p * dp, axis=0, keepdims=True)
+    ds = (p * (dp - delta) * SCORE_SCALE).astype(BF16)
+    dv_acc[:hi, :] += dot(p.astype(BF16), do, (1, 0))
+    dk_acc[:hi, :] += dot(ds, q, (1, 0))
+    dq = dot(ds, k_all, (0, 0))
+    cos_t, sin_t = rope_block(i, low_ref, high_ref)
+    dq32[rows, cols] = rotate(dq, cos_t, -sin_t).astype(BF16).astype(F32)
 
 
 SUBS = 4
@@ -193,8 +191,14 @@
     half = 2 * width
     peers = (right, left)
 
+    def local(sub):
+        start = sub * sub_rows
+        return pl.ds(start if isinstance(sub, int) else pl.multiple_of(start, sub_rows), sub_rows)
+
     def part(slot_ref, sub, with_extra):
-        return slot_ref.at[pl.ds(sub * sub_rows, sub_rows + (extra if with_extra and sub == SUBS - 1 else 0)), :]
+        if with_extra:
+            return slot_ref.at[pl.ds(sub * sub_rows, sub_rows + (extra if sub == SUBS - 1 else 0)), :]
+        return slot_ref.at[local(sub), :]
 
     def rs_copy(s, sub, way):
         return remote(part(rs_buf.at[way, s], sub, False), part(rs_buf.at[way, s + 1], sub, False),
@@ -216,27 +220,23 @@
     def dest_of(s, way):
         return (chip + n - 1 - s) % n if way == 0 else (chip + 1 + s) % n
 
-    def local(ref, sub):
-        return pl.ds(sub * sub_rows, sub_rows)
-
     for sub in range(SUBS):
         ready(sub)
         for way in range(2):
-            rs_buf[way, 0, local(rs_buf, sub), :] = my_part(dest_of(0, way), sub, way)
+            rs_buf[way, 0, local(sub), :] = my_part(dest_of(0, way), sub, way)
             rs_copy(0, sub, way).start()
 
-    def rs_step(s, carry):
-        for sub in range(SUBS):
-            for way in range(2):
-                term = my_part(dest_of(s, way), sub, way)
-                rs_copy(s - 1, sub, way).wait_recv()
-                rs_buf[way, s, local(rs_buf, sub), :] += term
-                rs_copy(s, sub, way).start()
-            if sub == 0:
-                rider(s)
+    def rs_step(k, carry):
+        s, sub = k // SUBS, k % SUBS
+        for way in range(2):
+            term = my_part(dest_of(s, way), sub, way)
+            rs_copy(s - 1, sub, way).wait_recv()
+            rs_buf[way, s, local(sub), :] += term
+            rs_copy(s, sub, way).start()
+        rider(s, sub)
         return carry
 
-    lax.fori_loop(1, n - 1, rs_step, 0)
+    lax.fori_loop(SUBS, SUBS * (n - 1), rs_step, 0)
 
     def out_copy(whose, s, sub, way):
         b = (chip + n - s) % n if way == 0 else (chip + s) % n
@@ -260,7 +260,7 @@
                 ag_copy(s, sub, way).start()
             sib_copy(s, sub, way).start()
         for way in range(2):
-            emit(0, s, sub, way, ag_buf[way, s, local(ag_buf, sub), :])
+            emit(0, s, sub, way, ag_buf[way, s, local(sub), :])
             if extra and sub == SUBS - 1:
                 gain_acc[0, way] += ag_buf[way, s, pl.ds(block, extra), :]
 
@@ -280,7 +280,7 @@
         terms = [my_part(chip, sub, way) for way in range(2)]
         for way in range(2):
             rs_copy(n - 2, sub, way).wait_recv()
-        finish(sub, [rs_buf[way, n - 1, local(rs_buf, sub), :] + terms[way] for way in range(2)])
+        finish(sub, [rs_buf[way, n - 1, local(sub), :] + terms[way] for way in range(2)])
         own_chunk(0, sub, True)
         if sub:
             sib_chunk(0, sub - 1)
@@ -410,28 +410,27 @@
     count = q_ref.shape[0] // ROWS
     per_wide = WIDE // ROWS
 
-    def ride(i, wides):
-        dout_copy(i).wait()
-
-        @pl.when(i + 1 < count)
-        def _():
-            dout_copy(i + 1).start()
-        do_blk[...] = dot(dout_rows[i % 2], wo_ref[...], (1, 1)).astype(BF16)
+    def ride(i, head, wides):
+        @pl.when(head == 0)
+        def _():
+            dout_copy(i).wait()
+            pl.when(i + 1 < count)(lambda: dout_copy(i + 1).start())
+            do_blk[...] = dot(dout_rows[i % 2], wo_ref[...], (1, 1)).astype(BF16)
         for c in wides:
             pl.when(i // per_wide == c)(
-                lambda c=c: attn_bwd_rows(i, c, do_blk, q_ref, k_ref, v_ref, low_ref, high_ref, x32, dk_acc, dv_acc))
+                lambda c=c: attn_bwd_rows(i, head, c, do_blk, q_ref, k_ref, v_ref, low_ref, high_ref, x32, dk_acc, dv_acc))
 
     early = n - 2
 
-    def rider(step):
-        ride(step - 1, range((early - 1) // per_wide + 1))
+    def rider(step, sub):
+        pl.when(sub % 2 == 0)(lambda: ride(step - 1, sub // 2, range((early - 1) // per_wide + 1)))
 
     def gather_rider(step):
-        @pl.when(step <= count - early)
-        def _():
-            ride(early - 1 + step, range(early // per_wide, count // per_wide))
-
-        @pl.when(step == count - early + 1)
+        @pl.when(step <= 2 * (count - early))
+        def _():
+            ride(early + (step - 1) // 2, (step - 1) % 2, range(early // per_wide, count // per_wide))
+
+        @pl.when(step == 2 * (count - early) + 1)
         def _():
             def turn_back(b, carry):
                 rows = pl.ds(pl.multiple_of(b * ROWS, ROWS), ROWS)
@@ -508,7 +507,7 @@
     for copy in weights + rows_copies + loads(0):
         copy.start()
     rhs[:, inner + 2 * HEAD_DIM:] = wqsib_ref[...].astype(BF16)
-    gain[...] = gain_ref[:, pl.ds(col, half)].astype(F32)
+    gain[...] = gain_ref[:, pl.ds(col, half)]
     for copy in weights:
         copy.wait()
     peers_ready()
@@ -530,12 +529,12 @@
             for copy in rows_copies:
                 copy.wait()
 
-    def rider(step):
-        @pl.when(step == 1)
-        def _():
-            for sub in range(SUBS):
-                prepare(sub)
-        pl.when(step - 1 < count)(lambda: weight_block(step - 1))
+    def rider(step, sub):
+        @pl.when((step == 1) & (sub == 0))
+        def _():
+            for own in range(SUBS):
+                prepare(own)
+        pl.when((sub == 1) & (step - 1 < count))(lambda: weight_block(step - 1))
 
     def gather_rider(step):
         pl.when(step + n - 3 < count)(lambda: weight_block(step + n - 3))
@@ -571,32 +570,34 @@
         for copy in stores(j):
             copy.wait()
     for way in range(2):
-        gsum_ref[core, way] = jnp.sum(gain_acc[0, way], axis=0, keepdims=True)
-        gsum_ref[1 - core, way] = jnp.sum(gain_acc[1, way], axis=0, keepdims=True)
+        for whose, start in ((0, col), (1, (1 - core) * half)):
+            cols = pl.ds(pl.multiple_of(start + way * width, 128), width)
+            gsum_ref[:, cols] = jnp.sum(gain_acc[whose, way], axis=0, keepdims=True)
 
 
 def final_kernel(*refs):
     half = len(refs) // 2
     for src, dst in zip(refs[:half], refs[half:]):
-        dst[...] = src[...]
-
-
-def final(out, gh, dw, dwo):
+        dst[...] = src[...].reshape(dst.shape)
+
+
+def final(out, gh, dw, dwo, gain_sum):
     seq, d = out.shape
     inner = dwo.shape[0]
-    steps = seq // ROWS
+    steps = seq // WIDE
     row = lambda a: pl.BlockSpec((a.shape[0] // steps, a.shape[1]), lambda j: (j, 0))
     part = lambda w, at: pl.BlockSpec((d // steps, w), lambda j: (j, at))
     shape = jax.ShapeDtypeStruct
     return pl.pallas_call(
         final_kernel, grid=(steps,),
-        in_specs=[row(out), row(gh), part(inner, 0), part(HEAD_DIM, inner // HEAD_DIM), part(HEAD_DIM, inner // HEAD_DIM + 1), row(dwo)],
-        out_specs=[row(out), row(gh), part(inner, 0), part(HEAD_DIM, 0), part(HEAD_DIM, 0), row(dwo)],
+        in_specs=[row(out), row(gh), part(inner, 0), part(HEAD_DIM, inner // HEAD_DIM), part(HEAD_DIM, inner // HEAD_DIM + 1), row(dwo),
+                  pl.BlockSpec((1, d), lambda j: (0, 0))],
+        out_specs=[row(out), row(gh), part(inner, 0), part(HEAD_DIM, 0), part(HEAD_DIM, 0), row(dwo), pl.BlockSpec((d,), lambda j: (0,))],
         out_shape=[shape(out.shape, BF16), shape(gh.shape, BF16), shape((d, inner), F32), shape((d, HEAD_DIM), F32),
-                   shape((d, HEAD_DIM), F32), shape(dwo.shape, F32)],
+                   shape((d, HEAD_DIM), F32), shape(dwo.shape, F32), shape((d,), F32)],
         compiler_params=pltpu.CompilerParams(vmem_limit_bytes=VMEM_LIMIT),
         cost_estimate=pl.CostEstimate(flops=seq * d, bytes_accessed=12 * seq * d, transcendentals=0),
-        name='final')(out, gh, dw, dw, dw, dwo)
+        name='final')(out, gh, dw, dw, dw, dwo, gain_sum)
 
 
 def out_sum(n, wo, q, k, v, low, high, x, dout):
@@ -630,7 +631,7 @@
     dma = pltpu.SemaphoreType.DMA
     return pl.pallas_call(
         functools.partial(grad_kernel, n),
-        out_shape=[shape((seq, d_model), BF16), shape((2, 2, 1, width), F32), shape((d_model, 2 * inner), F32), shape((inner, d_model), F32)],
+        out_shape=[shape((seq, d_model), BF16), shape((1, d_model), F32), shape((d_model, 2 * inner), F32), shape((inner, d_model), F32)],
         in_specs=[vmem] * 4 + [hbm] * 6, out_specs=[hbm, vmem, hbm, hbm],
         scratch_shapes=[pltpu.VMEM((2, seq, ROWS), BF16), pltpu.VMEM((2, seq, ROWS), BF16),
                         pltpu.VMEM((2, ROWS, 2 * inner), F32), pltpu.VMEM((2, inner, ROWS), F32), dma((2, 2)), dma((2, 2)),
@@ -656,14 +657,13 @@
         kv_index, core = tp_index // 2, tp_index % 2
         low, high = rope_tables(seq_len // ROWS)
         x, dout = hidden[0], grad_out[0]
-        gain = norm_gain[None, :]
         scalars = jnp.stack([kv_index, 1 - core])
-        n, q, k, v, wq32 = front(scalars, x, gain, w_query, w_key, w_value, low, high)
+        n, q, k, v, wq32, gain = front(scalars, x, norm_gain, w_query, w_key, w_value, low, high)
         wq_sib = lax.ppermute(wq32, 'tp', swap)
         out, o, dlhs = out_sum(chips, w_out, q, k, v, low, high, x, dout)
         gh, gain_sum, dw, dwo = grad_sum(chips, dlhs, o, wq_sib, gain, w_query, w_key, w_value, x, dout, n)
-        out, gh, grad_w_query, grad_w_key, grad_w_value, grad_w_out = final(out, gh, dw, dwo)
-        return out[None], gh[None], gain_sum.reshape(-1), grad_w_query, grad_w_key, grad_w_value, grad_w_out
+        out, gh, grad_w_query, grad_w_key, grad_w_value, grad_w_out, grad_gain = final(out, gh, dw, dwo, gain_sum)
+        return out[None], gh[None], grad_gain, grad_w_query, grad_w_key, grad_w_value, grad_w_out
 
     act_spec = P('dp', None, None)
     return jax.shard_map(

time: 481 us -> 480 us (level)
  no operation moved by 1% of the time
where the time goes in v1:
time: 480 us
  Pallas kernels  474 us (99%)
    pallas_call x1, Pallas kernels, out_sum(): pl.pallas_call(functools.partial(out_kernel, n), out_shape=[shape((seq, d...  223 us
    pallas_call x1, Pallas kernels, grad_sum(): pl.pallas_call(functools.partial(grad_kernel, n), out_shape=[shape((seq,...  214 us
    pallas_call x1, Pallas kernels, final(): pl.pallas_call(final_kernel, grid=(steps,), in_specs=[row(out), row(gh),...  20.2 us
    pallas_call x1, Pallas kernels, front(): pl.pallas_call(front_kernel, grid_spec=pltpu.PrefetchScalarGridSpec(num_s...  16 us
  transfers between devices with their start and end apart: 1, of which 0 were waited for; matrix products, arithmetic and copies ran while one was open for 0% of the time, Pallas kernels for 46%

profile of v1, /device:TPU:21, one launch (start us, length us, event | category | flops | bytes accessed | tf_op | source)
XLA Modules:
  0.0 479.7 jit_solution(1482212578915464985)
XLA Ops:
  0.7 0.6 pad_add_fusion.kv_ref
  1.2 16.0 %front.1 = (bf16[2048,2560]{1,0:T(8,128)(2,1)}, bf16[2048,256]{1,0:T(8,128)(2,1)}, bf16[2048,128]{1,0:T(8,128)(2,1)}, bf16[2048,128]{1,0:T(8,128)(2,1)}, f32[1280,256]{1,0:T(8,128)}, /*index=5*/f32[1,2560]{1,0:T(1,128)}) custom-call(s32[2]{0:T(128)} %pad_add_fusion.kv_ref, bf16[2048,2560]{1,0:T(8,128)(2,1)} %bitcast.6, bf16[2560]{0:T(1024)(128)(2,1)} %gain_ref.1, ...), custom_call_target="tpu_custom_call" | custom-call | flops 5368709120 | bytes 26214400 | tf_op jit(solution)/shard_map/front/pallas_call | solution.py:89
  17.2 4.8 collective-permute-start
  22.0 223.0 %out_sum.1 = (bf16[2048,2560]{1,0:T(8,128)(2,1)}, bf16[2048,256]{1,0:T(8,128)(2,1)}, bf16[2048,768]{1,0:T(8,128)(2,1)}) custom-call(bf16[256,2560]{1,0:T(8,128)(2,1)} %wo_ref.1, bf16[2048,256]{1,0:T(8,128)(2,1)} %get-tuple-element.27.q_ref, bf16[2048,128]{1,0:T(8,128)(2,1)} %get-tuple-element.28.k_ref, bf16[2048,128]{1,0:T(8,128)(2,1)} %get-tuple-element.29.v_ref, ...), custom_call_target="tpu_custom_call" | custom-call | flops 5368709120 | bytes 20971520 | tf_op jit(solution)/shard_map/out_sum/pallas_call | solution.py:611
  245.0 0.0 collective-permute-done.wqsib_ref
  245.0 214.3 %grad_sum.1 = (bf16[2048,2560]{1,0:T(8,128)(2,1)}, f32[1,2560]{1,0:T(1,128)}, f32[2560,512]{1,0:T(8,128)}, f32[256,2560]{1,0:T(8,128)}) custom-call(bf16[2048,768]{1,0:T(8,128)(2,1)} %get-tuple-element.31.lhs, bf16[2048,256]{1,0:T(8,128)(2,1)} %get-tuple-element.32.o_ref, f32[1280,256]{1,0:T(8,128)} %collective-permute-done.wqsib_ref, ...), custom_call_target="tpu_custom_call" | custom-call | flops 8053063680 | bytes 20971520 | tf_op jit(solution)/shard_map/grad_sum/pallas_call | solution.py:632
  459.3 20.2 %final.1 = (bf16[2048,2560]{1,0:T(8,128)(2,1)}, bf16[2048,2560]{1,0:T(8,128)(2,1)}, f32[2560,256]{1,0:T(8,128)}, f32[2560,128]{1,0:T(8,128)}, f32[2560,128]{1,0:...) custom-call(bf16[2048,2560]{1,0:T(8,128)(2,1)} %get-tuple-element.30.refs_0_, bf16[2048,2560]{1,0:T(8,128)(2,1)} %get-tuple-element.36.refs_1_, ...), custom_call_target="tpu_custom_call" | custom-call | flops 5242880 | bytes 62914560 | tf_op jit(solution)/shard_map/final/pallas_call | solution.py:591
Async XLA Ops:
  17.2 227.8 %collective-permute-start = (f32[1280,256]{1,0:T(8,128)}, f32[1280,256]{1,0:T(8,128)}, u32[]{:S(2)}, u32[]{:S(2)}) collective-permute-start(f32[1280,256]{1,0:T(8,128)} %get-tuple-element.33), channel_id=1, source_target_pairs={{0,1},{1,0},{2,3},{3,2},{4,5},{5,4},{6,7},{7,6},{8,9},{9,8},{10,11... | collective-permute-start | bytes 3932168 | tf_op jit(solution)/shard_map/ppermute | solution.py:662
